TPU v7x, 128 devices: a whole 4x4x4 slice. The times are simulated.
128 devices in a mesh: lat: 16 (over z_lo, y, core), lon: 8 (over z_hi, x).
Axes of the slice: x: 4, y: 4, z: 4 (z_hi: 2, z_lo: 2; z = z_hi * 2 + z_lo), core: 2. Of those that a mesh axis runs over, the one named last changes fastest.
Arguments:
- tokens: bfloat16 [4, 128, 256, 1024], P(None, 'lat', 'lon'), may hold values from -6 to 6
- qkv_weight: bfloat16 [3072, 1024], P(('lat', 'lon')), may hold values from -0.1875 to 0.1875
- proj_weight: bfloat16 [1024, 1024], P(('lat', 'lon')), may hold values from -0.1875 to 0.1875
- up_weight: bfloat16 [4096, 1024], P(('lat', 'lon')), may hold values from -0.1875 to 0.1875
- down_weight: bfloat16 [4096, 1024], P(('lat', 'lon')), may hold values from -0.09375 to 0.09375
- bias_table: float32 [225, 16], replicated, may hold values from -3 to 220
- sea_mask: int32 [128, 256], replicated, may hold values 0 or 1
Outputs:
- block_out: bfloat16 [4, 128, 256, 1024], P(None, 'lat', 'lon')
All inputs are finite; a program needn't handle non-finite values.
Results may differ from a plain program's by a relative error of at most 0.012.
Values may be sent and summed in bfloat16 or wider, within the bound.
No kernel may reach another device: no remote copies, remote signals or barrier semaphores. Data moves between devices by JAX's collectives and lax.ppermute only.
A program may use at most 128 MiB of HBM per device.

v0:
```python
import jax
import jax.numpy as jnp
from jax import lax
from jax.sharding import PartitionSpec as P


def from_behind(value, axis, steps):
    count = lax.axis_size(axis)
    pairs = [(source, (source + steps) % count) for source in range(count)]
    return lax.ppermute(value, axis, pairs)


def sent_together(arrays, axis, dim, along):
    ends, at = ([], 0)
    for a in arrays[:-1]:
        at += a.shape[along]
        ends.append(at)
    both = jnp.concatenate(arrays, axis=along)
    return tuple(jnp.split(lax.all_gather(both, axis, axis=dim, tiled=True), ends, axis=along))


def layer_norm(values):
    widened = values.astype(jnp.float32)
    centre = jnp.mean(widened, axis=-1, keepdims=True)
    spread = jnp.mean(jnp.square(widened - centre), axis=-1, keepdims=True)
    return ((widened - centre) * lax.rsqrt(spread + 1e-05)).astype(jnp.bfloat16)


def offsets_table():
    cell_ids = jnp.arange(64, dtype=jnp.int32)
    row_of = cell_ids // 8
    col_of = cell_ids % 8
    return (row_of[:, None] - row_of[None, :] + 7) * 15 + (col_of[:, None] - col_of[None, :] + 7)


def row_region(row_ids, total_rows):
    return jnp.where(row_ids < 4, 2, jnp.where(row_ids >= total_rows - 4, 1, 0)).astype(jnp.int32)


def window_attention(queries, pair_cells, row_start, col_start, sea_mask, pos_bias):
    batch_size, row_count, col_count, feat_width = queries.shape
    head_count = pos_bias.shape[0]
    head_size = feat_width // head_count
    lat_cells, lon_cells = sea_mask.shape
    down_count = row_count // 8
    across_count = col_count // 8
    window_count = down_count * across_count

    def to_windows(values):
        last_dim = values.shape[-1]
        shaped = values.reshape(batch_size, down_count, 8, across_count, 8, last_dim)
        return shaped.transpose(0, 1, 3, 2, 4, 5).reshape(batch_size, window_count, 64, last_dim)

    query_win = to_windows(queries)
    pair_win = to_windows(pair_cells)
    grid_rows = (row_start + jnp.arange(row_count, dtype=jnp.int32)) % lat_cells
    region = row_region(grid_rows, lat_cells).reshape(down_count, 8)
    region = jnp.broadcast_to(region[:, None, :, None], (down_count, across_count, 8, 8)).reshape(
        window_count, 64
    )
    sea_tiled = jnp.tile(sea_mask, (2, 2))
    sea_keep = lax.dynamic_slice(
        sea_tiled, (row_start % lat_cells, col_start % lon_cells), (row_count, col_count)
    )
    sea_keep = (
        sea_keep.reshape(down_count, 8, across_count, 8)
        .transpose(0, 2, 1, 3)
        .reshape(window_count, 64)
        == 1
    )
    same_cell = jnp.eye(64, dtype=bool)
    allowed = (region[:, :, None] == region[:, None, :]) & (sea_keep[:, None, :] | same_cell[None])
    group_width = 4 * head_size
    score_scale = head_size ** (-0.5)

    def one_group(group_index):
        first_col = group_index * group_width
        split_shape = (batch_size, window_count, 64, 4, head_size)
        query_part = lax.dynamic_slice_in_dim(query_win, first_col, group_width, 3).reshape(
            split_shape
        )
        key_part = lax.dynamic_slice_in_dim(pair_win, first_col, group_width, 3).reshape(
            split_shape
        )
        value_part = lax.dynamic_slice_in_dim(
            pair_win, feat_width + first_col, group_width, 3
        ).reshape(split_shape)
        bias_part = lax.dynamic_slice_in_dim(pos_bias, group_index * 4, 4, 0)
        scores = jnp.einsum(
            "bsqhd,bskhd->bshqk", query_part, key_part, preferred_element_type=jnp.float32
        )
        scores = scores * score_scale + bias_part[None, None]
        scores = jnp.where(allowed[None, :, None], scores, -1e30)
        row_top = jnp.max(scores, axis=-1, keepdims=True)
        weights = jnp.exp(scores - row_top)
        attn_probs = (weights / jnp.sum(weights, axis=-1, keepdims=True)).astype(jnp.bfloat16)
        context = jnp.einsum(
            "bshqk,bskhd->bsqhd", attn_probs, value_part, preferred_element_type=jnp.float32
        )
        return context.astype(jnp.bfloat16).reshape(batch_size, window_count, 64, group_width)

    groups = lax.map(one_group, jnp.arange(head_count // 4, dtype=jnp.int32))
    context = jnp.transpose(groups, (1, 2, 3, 0, 4)).reshape(
        batch_size, down_count, across_count, 8, 8, feat_width
    )
    return context.transpose(0, 1, 3, 2, 4, 5).reshape(batch_size, row_count, col_count, feat_width)


def per_device(tokens, qkv_weight, proj_weight, up_weight, down_weight, bias_table, sea_mask):
    batch_size, lat_rows, lon_cols, feat_width = tokens.shape
    head_count = bias_table.shape[1]
    row_base = lax.axis_index("lat") * lat_rows
    col_base = lax.axis_index("lon") * lon_cols
    offset_ids = offsets_table().reshape(-1)
    one_hot = (
        offset_ids[:, None] == jnp.arange(bias_table.shape[0], dtype=jnp.int32)[None, :]
    ).astype(jnp.float32)
    pos_bias = jnp.dot(one_hot, bias_table, precision=lax.Precision.HIGHEST)
    pos_bias = pos_bias.reshape(64, 64, head_count).transpose(2, 0, 1)
    normed = layer_norm(tokens)
    arrived = from_behind(normed[:, :4], "lat", -1)
    rolled_rows = jnp.concatenate([normed[:, 4:], arrived], axis=1)
    arrived_cols = from_behind(rolled_rows[:, :, :4], "lon", -1)
    feed_cells = jnp.concatenate([rolled_rows[:, :, 4:], arrived_cols], axis=2)
    feed_flat = feed_cells.reshape(-1, feat_width)
    projected = lax.dot_general(
        feed_flat,
        lax.all_gather(qkv_weight, ("lat", "lon"), axis=0, tiled=True),
        (((1,), (1,)), ((), ())),
        preferred_element_type=jnp.float32,
    ).astype(jnp.bfloat16)
    projected = projected.reshape(batch_size, lat_rows, lon_cols, 3 * feat_width)
    queries = projected[..., :feat_width]
    pair_cells = projected[..., feat_width:]
    rolled_context = window_attention(
        queries, pair_cells, row_base + 4, col_base + 4, sea_mask, pos_bias
    )
    came_cols = from_behind(rolled_context[:, :, lon_cols - 4 :], "lon", 1)
    back_cols = jnp.concatenate([came_cols, rolled_context[:, :, : lon_cols - 4]], axis=2)
    came_rows = from_behind(back_cols[:, lat_rows - 4 :], "lat", 1)
    context = jnp.concatenate([came_rows, back_cols[:, : lat_rows - 4]], axis=1)
    context_flat = context.reshape(-1, feat_width)
    attention_out = lax.dot_general(
        context_flat,
        lax.all_gather(proj_weight, ("lat", "lon"), axis=0, tiled=True),
        (((1,), (1,)), ((), ())),
        preferred_element_type=jnp.float32,
    )
    attended = (tokens.reshape(-1, feat_width).astype(jnp.float32) + attention_out).astype(
        jnp.bfloat16
    )
    normed_two = layer_norm(attended)
    up_part, down_part = sent_together((up_weight, down_weight), ("lat", "lon"), 0, 1)
    hidden = lax.dot_general(
        normed_two, up_part, (((1,), (1,)), ((), ())), preferred_element_type=jnp.float32
    )
    hidden = jax.nn.gelu(hidden).astype(jnp.bfloat16)
    hidden_sum = jnp.dot(hidden, down_part, preferred_element_type=jnp.float32)
    result = (attended.astype(jnp.float32) + hidden_sum).astype(jnp.bfloat16)
    return result.reshape(tokens.shape)


def solution(mesh):
    placed = (
        P(None, "lat", "lon", None),
        P(("lat", "lon"), None),
        P(("lat", "lon"), None),
        P(("lat", "lon"), None),
        P(("lat", "lon"), None),
        P(),
        P(),
    )
    return jax.shard_map(
        per_device,
        mesh=mesh,
        in_specs=placed,
        out_specs=P(None, "lat", "lon", None),
        check_vma=False,
    )
```

profile of v0, /device:TPU:1, one launch (start us, length us, event | category | flops | bytes accessed | tf_op | source)
XLA Modules:
  0.0 980.6 jit_solution(1794347280123285395)
XLA Ops:
  6.5 0.7 all-gather.4.cloned.1.call-update
  7.3 0.7 all-gather.6.cloned.1.call-update
  8.1 1.5 pad_maximum_fusion.3
  9.6 1.9 convert_reduce_fusion.1
  11.6 2.3 multiply_reduce_fusion
  13.9 0.6 multiply_convert_fusion
  14.5 1.2 fusion.79
  15.6 1.4 collective-permute-start
  17.8 2.6 fusion.48
  20.6 1.0 copy.26
  21.7 9.3 collective-permute-done
  31.1 7.6 collective-permute-start.1
  38.7 0.5 slice_maximum_fusion
  39.3 4.4 collective-permute-done.1
  44.1 274.7 %all-gather.4.cloned.1.call-done = bf16[3072,1024]{1,0:T(8,128)(2,1)} async-done(((bf16[24,1024]{1,0:T(8,128)(2,1)}), bf16[3072,1024]{1,0:T(8,128)(2,1)}) %all-gather.4.cloned.1.call-update) | async-done | bytes 6291472 | tf_op jit(solution)/shard_map/all_gather | solution.py:128
  318.8 9.7 convolution_convert_fusion.1
  328.5 1.5 copy_bitcast_fusion.2
  330.0 2.3 copy_bitcast_fusion
  332.4 45.6 %while.13 = (s32[]{:T(128)}, bf16[4,4,4,64,256]{3,4,2,1,0:T(8,128)(2,1)}, s32[4]{0:T(128)S(1)}, bf16[4,4,64,2048]{3,2,1,0:T(8,128)(2,1)}, bf16[4,4,64,1024]{3,2,...) while((s32[]{:T(128)}, ...), condition=%wide.region_5.6_spmd.clone, body=%wide.region_2.5_spmd.clone.sunk | while | flops 69255248 | bytes 12326224 | solution.py:102
  332.4 0.6 dynamic_slice.50
  333.6 1.5 constant_dynamic-slice_fusion.6
  335.5 0.4 reshape.231
  336.6 0.9 constant_dynamic-slice_fusion.7
  337.6 2.6 fusion.94
  340.2 0.5 copy.60
  340.7 2.0 convolution_convert_fusion.3
  342.7 1.1 constant_dynamic-update-slice_fusion.2
  343.8 0.6 dynamic_slice.50
  345.0 1.5 constant_dynamic-slice_fusion.6
  346.9 0.4 reshape.231
  348.0 0.9 constant_dynamic-slice_fusion.7
  349.0 2.6 fusion.94
  351.6 0.5 copy.60
  352.1 2.0 convolution_convert_fusion.3
  354.1 1.1 constant_dynamic-update-slice_fusion.2
  355.2 0.6 dynamic_slice.50
  356.4 1.5 constant_dynamic-slice_fusion.6
  358.3 0.4 reshape.231
  359.4 0.9 constant_dynamic-slice_fusion.7
  360.4 2.6 fusion.94
  363.0 0.5 copy.60
  363.5 2.0 convolution_convert_fusion.3
  365.5 1.1 constant_dynamic-update-slice_fusion.2
  366.6 0.6 dynamic_slice.50
  367.9 1.5 constant_dynamic-slice_fusion.6
  370.8 0.9 constant_dynamic-slice_fusion.7
  371.8 2.6 fusion.94
  374.4 0.5 copy.60
  374.9 2.0 convolution_convert_fusion.3
  376.9 1.0 constant_dynamic-update-slice_fusion.2
  378.0 5.5 copy.28
  383.5 2.7 reshape.220
  386.2 1.8 copy_bitcast_fusion.1
  388.2 0.9 collective-permute-start.2
  389.1 10.5 %collective-permute-done.2 = bf16[4,8,4,1024]{3,2,1,0:T(4,128)(2,1)S(1)} collective-permute-done((bf16[4,8,4,1024]{3,2,1,0:T(4,128)(2,1)S(1)}, bf16[4,8,4,1024]{3,2,1,0:T(4,128)(2,1)S(1)}, u32[]{:S(2)}, u32[]{:S(2)}) %collective-permute-start.2) | collective-permute-done | bytes 262176 | tf_op jit(solution)/shard_map/ppermute | solution.py:10
  400.0 1.5 collective-permute-start.3
  401.5 11.7 %collective-permute-done.3 = bf16[4,4,32,1024]{3,2,1,0:T(8,128)(2,1)S(1)} collective-permute-done((bf16[4,4,32,1024]{3,2,1,0:T(8,128)(2,1)S(1)}, bf16[4,4,32,1024]{3,2,1,0:T(8,128)(2,1)S(1)}, u32[]{:S(2)}, u32[]{:S(2)}) %collective-permute-start.3) | collective-permute-done | bytes 1048608 | tf_op jit(solution)/shard_map/ppermute | solution.py:10
  413.3 1.8 fusion.62
  415.1 211.3 %all-gather.6.cloned.1.call-done = bf16[1024,1024]{1,0:T(8,128)(2,1)} async-done(((bf16[8,1024]{1,0:T(8,128)(2,1)}), bf16[1024,1024]{1,0:T(8,128)(2,1)}) %all-gather.6.cloned.1.call-update) | async-done | bytes 2097168 | tf_op jit(solution)/shard_map/all_gather | solution.py:145
  626.3 4.7 convert_reduce_fusion
  631.0 1.3 copy-done.4
  632.4 0.7 fusion.44
  633.1 314.2 %all-gather.8.cloned.1.call-done = bf16[4096,2048]{1,0:T(8,128)(2,1)} async-done(((bf16[32,2048]{1,0:T(8,128)(2,1)}), bf16[4096,2048]{1,0:T(8,128)(2,1)}) %all-gather.8.cloned.1.call-update) | async-done | bytes 16777232 | tf_op jit(solution)/shard_map/all_gather | solution.py:19
  947.3 26.8 %fusion.46 = bf16[1024,1024]{1,0:T(8,128)(2,1)} fusion(bf16[1024,1024]{1,0:T(8,128)(2,1)} %copy-done.4, bf16[4096,2048]{1,0:T(8,128)(2,1)} %all-gather.8.cloned.1.call-done, f32[1024]{0:T(1024)S(1)} %add_rsqrt_fusion.1, f32[1024]{0:T(1024)S(1)} %broadcast_multiply_fusion.1), kind=kOutput, calls=%fused_computation.47 | convolution fusion | flops 17224957952 | bytes 23076864 | tf_op jit(solution)/shard_map/dot_general | solution.py:158
  (48 shorter events, 4.6 us)
Async XLA Ops:
  6.5 11.3 %copy-start = (f32[225,16]{0,1:T(8,128)S(1)}, f32[225,16]{0,1:T(8,128)}, u32[]{:S(2)}) copy-start(f32[225,16]{0,1:T(8,128)} %param.14) | copy-start | bytes 43204
  6.5 7.3 copy-start.2
  6.5 312.3 %all-gather.4.cloned.1.call-start = ((), (), s32[]{:S(2)}) async-start(), calls=%async_computation | async-start | bytes 6340608 | tf_op jit(solution)/shard_map/all_gather | solution.py:128
  7.3 619.1 %all-gather.6.cloned.1.call-start = ((), (), s32[]{:S(2)}) async-start(), calls=%async_computation.1 | async-start | bytes 2113536 | tf_op jit(solution)/shard_map/all_gather | solution.py:145
  8.0 939.3 %all-gather.8.cloned.1.call-start = ((), (), s32[]{:S(2)}) async-start(), calls=%async_computation.2 | async-start | bytes 16908288 | tf_op jit(solution)/shard_map/all_gather | solution.py:19
  13.9 3.1 copy-start.5
  15.6 15.4 %collective-permute-start = (bf16[4,4,32,1024]{3,2,1,0:T(8,128)(2,1)}, bf16[4,4,32,1024]{3,2,1,0:T(8,128)(2,1)S(1)}, u32[]{:S(2)}, u32[]{:S(2)}) collective-permute-start(bf16[4,4,32,1024]{3,2,1,0:T(8,128)(2,1)} %get-tuple-element.142), channel_id=1, source_target_pairs={{0,120},{8,0},{16,8},{24,16},{32,24},{40,32},{48,40},{56,48},{64,5... | collective-permute-start | bytes 3145736 | tf_op jit(solution)/shard_map/ppermute | solution.py:10
  31.1 12.6 %collective-permute-start.1 = (bf16[4,8,4,1024]{3,2,1,0:T(4,128)(2,1)S(1)}, bf16[4,8,4,1024]{3,2,1,0:T(4,128)(2,1)S(1)}, u32[]{:S(2)}, u32[]{:S(2)}) collective-permute-start(bf16[4,8,4,1024]{3,2,1,0:T(4,128)(2,1)S(1)} %pad_maximum_fusion.2), channel_id=1, source_target_pairs={{0,7},{1,0},{2,1},{3,2},{4,3},{5,4},{6,5},{7,6},{8,15},{9,8},{10,9... | collective-permute-start | bytes 786440 | tf_op jit(solution)/shard_map/ppermute | solution.py:10
  388.2 11.4 %collective-permute-start.2 = (bf16[4,8,4,1024]{3,2,1,0:T(4,128)(2,1)S(1)}, bf16[4,8,4,1024]{3,2,1,0:T(4,128)(2,1)S(1)}, u32[]{:S(2)}, u32[]{:S(2)}) collective-permute-start(bf16[4,8,4,1024]{3,2,1,0:T(4,128)(2,1)S(1)} %slice.46), channel_id=1, source_target_pairs={{0,1},{1,2},{2,3},{3,4},{4,5},{5,6},{6,7},{7,0},{8,9},{9,10},{10,1... | collective-permute-start | bytes 786440 | tf_op jit(solution)/shard_map/ppermute | solution.py:10
  399.6 226.7 %copy-start.3 = (bf16[4,8,32,1024]{3,2,1,0:T(8,128)(2,1)S(1)}, bf16[4,8,32,1024]{3,2,1,0:T(8,128)(2,1)}, u32[]{:S(2)}) copy-start(bf16[4,8,32,1024]{3,2,1,0:T(8,128)(2,1)} %param.9) | copy-start | bytes 6291460
  400.0 13.2 %collective-permute-start.3 = (bf16[4,4,32,1024]{3,2,1,0:T(8,128)(2,1)S(1)}, bf16[4,4,32,1024]{3,2,1,0:T(8,128)(2,1)S(1)}, u32[]{:S(2)}, u32[]{:S(2)}) collective-permute-start(bf16[4,4,32,1024]{3,2,1,0:T(8,128)(2,1)S(1)} %fusion.68), channel_id=1, source_target_pairs={{0,8},{8,16},{16,24},{24,32},{32,40},{40,48},{48,56},{56,64},{64,7... | collective-permute-start | bytes 3145736 | tf_op jit(solution)/shard_map/ppermute | solution.py:10
  631.0 1.4 copy-start.4
  947.3 26.8 %copy-start.1 = (f32[225,16]{0,1:T(8,128)S(1)}, f32[225,16]{0,1:T(8,128)}, u32[]{:S(2)}) copy-start(f32[225,16]{0,1:T(8,128)} %param.14) | copy-start | bytes 43204
Sparse Core Ops, SparseCore 0:
  9.0 309.7 all-gather.3
  320.5 305.8 all-gather.5
  628.0 319.1 all-gather.7
where the time goes:
time: 981 us
  waiting for transfers between devices  838 us (85%)
  matrix products  62.2 us (6%)
  local copies, waits for them, and re-layouts  39.9 us (4%)
  between operations  13.3 us (1%)
  starting transfers between devices  11.5 us (1%)
  other arithmetic  10.9 us (1%)
    all_gather x1, waiting for transfers between devices, sent_together(): lax.all_gather(both, axis, axis=dim, tiled=True)  314 us
    all_gather x1, waiting for transfers between devices, per_device(): lax.all_gather(qkv_weight, ('lat', 'lon'), axis=0, tiled=True)  275 us
    all_gather x1, waiting for transfers between devices, per_device(): lax.all_gather(proj_weight, ('lat', 'lon'), axis=0, tiled=True)  211 us
    ppermute x4, waiting for transfers between devices, from_behind(): return lax.ppermute(value, axis, pairs)  36 us
    dot_general x1, matrix products, per_device(): hidden_sum = jnp.dot(hidden, down_part, preferred_element_type=jnp.float32)  26.8 us
  transfers between devices with their start and end apart: 7, of which 7 were waited for; matrix products, arithmetic and copies ran while one was open for 9% of the time, Pallas kernels for 0%

commit v1 on v0

--- a/solution.py
+++ b/solution.py
@@ -125,7 +125,12 @@
     feed_flat = feed_cells.reshape(-1, feat_width)
     projected = lax.dot_general(
         feed_flat,
-        lax.all_gather(qkv_weight, ("lat", "lon"), axis=0, tiled=True),
+        jnp.concatenate(
+            lax.all_to_all(
+                jnp.stack([qkv_weight] * lax.axis_size(("lat", "lon"))), ("lat", "lon"), 0, 0
+            ),
+            axis=0,
+        ),
         (((1,), (1,)), ((), ())),
         preferred_element_type=jnp.float32,
     ).astype(jnp.bfloat16)

time: 981 us -> 721 us (0.73)
  waiting for transfers between devices: 838 us -> 565 us
  starting transfers between devices: 11.5 us -> 21.8 us
    all_gather x1 -> x0, waiting for transfers between devices: 275 us -> none  [per_device(): lax.all_gather(qkv_weight, ('lat', 'lon'), axis=0, tiled=True)]
    ppermute x4, waiting for transfers between devices: 36 us -> 101 us  [from_behind(): return lax.ppermute(value, axis, pairs)]
    all_gather x1, waiting for transfers between devices: 211 us -> 149 us  [per_device(): lax.all_gather(proj_weight, ('lat', 'lon'), axis=0, tiled=True)]
    all_to_all x0 -> x1, starting transfers between devices: none -> 11.9 us  [per_device(): lax.all_to_all(jnp.stack([qkv_weight] * lax.axis_size(('lat', 'lon'))), (...]
  transfers between devices with their start and end apart: 7 -> 7, of which waited for: 7 -> 6; matrix products, arithmetic and copies ran while one was open for 9% -> 12% of each run, Pallas kernels for 0% -> 0%
where the time goes in v1:
time: 721 us; the launch traced here: 720 us
  waiting for transfers between devices  565 us (78%)
  matrix products  62.2 us (9%)
  local copies, waits for them, and re-layouts  44.2 us (6%)
  starting transfers between devices  21.8 us (3%)
  between operations  13.6 us (2%)
  other arithmetic  7.69 us (1%)
    all_gather x1, waiting for transfers between devices, sent_together(): lax.all_gather(both, axis, axis=dim, tiled=True)  314 us
    all_gather x1, waiting for transfers between devices, per_device(): lax.all_gather(proj_weight, ('lat', 'lon'), axis=0, tiled=True)  149 us
    ppermute x4, waiting for transfers between devices, from_behind(): return lax.ppermute(value, axis, pairs)  101 us
    dot_general x1, matrix products, per_device(): hidden_sum = jnp.dot(hidden, down_part, preferred_element_type=jnp.float32)  26.8 us
  transfers between devices with their start and end apart: 7, of which 6 were waited for; matrix products, arithmetic and copies ran while one was open for 12% of the time, Pallas kernels for 0%

profile of v1, /device:TPU:1, one launch (start us, length us, event | category | flops | bytes accessed | tf_op | source)
XLA Modules:
  0.0 720.2 jit_solution(15055308636836806585)
XLA Ops:
  6.5 0.7 all-gather.3.cloned.1.call-update
  7.3 1.5 pad_maximum_fusion.3
  8.9 4.2 stack.2
  13.1 11.9 %all-to-all-start = ((bf16[128,24,1024]{2,1,0:T(8,128)(2,1)}), bf16[128,24,1024]{2,1,0:T(8,128)(2,1)}, u32[]{:S(2)}, u32[]{:S(2)}) async-start(bf16[128,24,1024]{2,1,0:T(8,128)(2,1)} %stack.2), calls=%async_computation | async-start | bytes 12582912 | tf_op jit(solution)/shard_map/all_to_all | solution.py:129
  25.4 0.7 multiply_reduce_fusion
  26.1 0.6 multiply_convert_fusion
  26.7 1.2 fusion.79
  27.8 1.1 collective-permute-start
  29.8 2.6 fusion.48
  32.6 1.0 copy.26
  33.6 76.9 %collective-permute-done = bf16[4,4,32,1024]{3,2,1,0:T(8,128)(2,1)S(1)} collective-permute-done((bf16[4,4,32,1024]{3,2,1,0:T(8,128)(2,1)}, bf16[4,4,32,1024]{3,2,1,0:T(8,128)(2,1)S(1)}, u32[]{:S(2)}, u32[]{:S(2)}) %collective-permute-start) | collective-permute-done | bytes 1048608 | tf_op jit(solution)/shard_map/ppermute | solution.py:10
  110.6 6.6 collective-permute-start.1
  117.3 0.5 slice_maximum_fusion
  117.8 2.8 collective-permute-done.1
  121.0 9.7 %convolution_convert_fusion.1 = bf16[1024,3072]{1,0:T(8,128)(2,1)S(1)} fusion(bf16[1024,1024]{1,0:T(8,128)(2,1)S(1)} %bitcast.74, bf16[3072,1024]{1,0:T(8,128)(2,1)} %bitcast.2), kind=kOutput, calls=%fused_computation.42 | convolution fusion | flops 6445596672 | bytes 14680064 | tf_op jit(solution)/shard_map/dot_general | solution.py:126
  130.7 1.5 copy_bitcast_fusion.2
  132.2 2.3 copy_bitcast_fusion
  134.6 45.6 %while.13 = (s32[]{:T(128)}, bf16[4,4,4,64,256]{3,4,2,1,0:T(8,128)(2,1)}, s32[4]{0:T(128)S(1)}, bf16[4,4,64,2048]{3,2,1,0:T(8,128)(2,1)}, bf16[4,4,64,1024]{3,2,...) while((s32[]{:T(128)}, ...), condition=%wide.region_5.6_spmd.clone, body=%wide.region_2.5_spmd.clone.sunk | while | flops 69255248 | bytes 12326224 | solution.py:102
  134.6 0.6 dynamic_slice.50
  135.8 1.5 constant_dynamic-slice_fusion.6
  137.7 0.4 reshape.237
  138.7 0.9 constant_dynamic-slice_fusion.7
  139.8 2.6 fusion.94
  142.4 0.5 copy.60
  142.8 2.0 convolution_convert_fusion.3
  144.9 1.1 constant_dynamic-update-slice_fusion.2
  146.0 0.6 dynamic_slice.50
  147.2 1.5 constant_dynamic-slice_fusion.6
  148.7 0.4 reshape.236
  149.1 0.4 reshape.237
  150.2 0.9 constant_dynamic-slice_fusion.7
  151.2 2.6 fusion.94
  153.8 0.5 copy.60
  154.3 2.0 convolution_convert_fusion.3
  156.3 1.1 constant_dynamic-update-slice_fusion.2
  157.4 0.6 dynamic_slice.50
  158.6 1.5 constant_dynamic-slice_fusion.6
  160.5 0.4 reshape.237
  161.6 0.9 constant_dynamic-slice_fusion.7
  162.6 2.6 fusion.94
  165.2 0.5 copy.60
  165.7 2.0 convolution_convert_fusion.3
  167.7 1.1 constant_dynamic-update-slice_fusion.2
  168.8 0.6 dynamic_slice.50
  170.0 1.5 constant_dynamic-slice_fusion.6
  171.9 0.4 reshape.237
  172.9 0.9 constant_dynamic-slice_fusion.7
  174.0 2.6 fusion.94
  176.6 0.5 copy.60
  177.1 2.0 convolution_convert_fusion.3
  179.1 1.1 constant_dynamic-update-slice_fusion.2
  180.1 5.5 copy.28
  185.7 2.7 reshape.226
  188.4 1.8 copy_bitcast_fusion.1
  190.4 9.5 %collective-permute-done.2 = bf16[4,8,4,1024]{3,2,1,0:T(4,128)(2,1)S(1)} collective-permute-done((bf16[4,8,4,1024]{3,2,1,0:T(4,128)(2,1)S(1)}, bf16[4,8,4,1024]{3,2,1,0:T(4,128)(2,1)S(1)}, u32[]{:S(2)}, u32[]{:S(2)}) %collective-permute-start.2) | collective-permute-done | bytes 262176 | tf_op jit(solution)/shard_map/ppermute | solution.py:10
  200.4 2.1 collective-permute-start.3
  202.5 11.7 %collective-permute-done.3 = bf16[4,4,32,1024]{3,2,1,0:T(8,128)(2,1)S(1)} collective-permute-done((bf16[4,4,32,1024]{3,2,1,0:T(8,128)(2,1)S(1)}, bf16[4,4,32,1024]{3,2,1,0:T(8,128)(2,1)S(1)}, u32[]{:S(2)}, u32[]{:S(2)}) %collective-permute-start.3) | collective-permute-done | bytes 1048608 | tf_op jit(solution)/shard_map/ppermute | solution.py:10
  214.2 1.8 fusion.62
  216.0 149.3 %all-gather.3.cloned.1.call-done = bf16[1024,1024]{1,0:T(8,128)(2,1)} async-done(((bf16[8,1024]{1,0:T(8,128)(2,1)}), bf16[1024,1024]{1,0:T(8,128)(2,1)}) %all-gather.3.cloned.1.call-update) | async-done | bytes 2097168 | tf_op jit(solution)/shard_map/all_gather | solution.py:150
  365.3 4.7 convert_reduce_fusion
  370.0 1.3 copy-done.4
  371.3 0.7 fusion.44
  372.0 314.5 %all-gather.5.cloned.1.call-done = bf16[4096,2048]{1,0:T(8,128)(2,1)} async-done(((bf16[32,2048]{1,0:T(8,128)(2,1)}), bf16[4096,2048]{1,0:T(8,128)(2,1)}) %all-gather.5.cloned.1.call-update) | async-done | bytes 16777232 | tf_op jit(solution)/shard_map/all_gather | solution.py:19
  686.5 26.8 %fusion.46 = bf16[1024,1024]{1,0:T(8,128)(2,1)} fusion(bf16[1024,1024]{1,0:T(8,128)(2,1)} %copy-done.4, bf16[4096,2048]{1,0:T(8,128)(2,1)} %all-gather.5.cloned.1.call-done, f32[1024]{0:T(1024)S(1)} %add_rsqrt_fusion.1, f32[1024]{0:T(1024)S(1)} %broadcast_multiply_fusion.1), kind=kOutput, calls=%fused_computation.47 | convolution fusion | flops 17224957952 | bytes 23076864 | tf_op jit(solution)/shard_map/dot_general | solution.py:163
  (48 shorter events, 4.2 us)
Async XLA Ops:
  6.5 23.3 %copy-start = (f32[225,16]{0,1:T(8,128)S(1)}, f32[225,16]{0,1:T(8,128)}, u32[]{:S(2)}) copy-start(f32[225,16]{0,1:T(8,128)} %param.14) | copy-start | bytes 43204
  6.5 358.8 %all-gather.3.cloned.1.call-start = ((), (), s32[]{:S(2)}) async-start(), calls=%async_computation.1 | async-start | bytes 2113536 | tf_op jit(solution)/shard_map/all_gather | solution.py:150
  7.3 679.3 %all-gather.5.cloned.1.call-start = ((), (), s32[]{:S(2)}) async-start(), calls=%async_computation.2 | async-start | bytes 16908288 | tf_op jit(solution)/shard_map/all_gather | solution.py:19
  13.1 11.9 %copy-start.2 = (bf16[4,8,32,1024]{3,2,1,0:T(8,128)(2,1)S(1)}, bf16[4,8,32,1024]{3,2,1,0:T(8,128)(2,1)}, u32[]{:S(2)}) copy-start(bf16[4,8,32,1024]{3,2,1,0:T(8,128)(2,1)} %param.9) | copy-start | bytes 6291460
  13.1 107.8 %all-to-all-start = ((bf16[128,24,1024]{2,1,0:T(8,128)(2,1)}), bf16[128,24,1024]{2,1,0:T(8,128)(2,1)}, u32[]{:S(2)}, u32[]{:S(2)}) async-start(bf16[128,24,1024]{2,1,0:T(8,128)(2,1)} %stack.2), calls=%async_computation | async-start | bytes 12582912 | tf_op jit(solution)/shard_map/all_to_all | solution.py:129
  26.1 2.9 copy-start.5
  27.8 82.7 %collective-permute-start = (bf16[4,4,32,1024]{3,2,1,0:T(8,128)(2,1)}, bf16[4,4,32,1024]{3,2,1,0:T(8,128)(2,1)S(1)}, u32[]{:S(2)}, u32[]{:S(2)}) collective-permute-start(bf16[4,4,32,1024]{3,2,1,0:T(8,128)(2,1)} %get-tuple-element.142), channel_id=1, source_target_pairs={{0,120},{8,0},{16,8},{24,16},{32,24},{40,32},{48,40},{56,48},{64,5... | collective-permute-start | bytes 3145736 | tf_op jit(solution)/shard_map/ppermute | solution.py:10
  110.6 9.9 %collective-permute-start.1 = (bf16[4,8,4,1024]{3,2,1,0:T(4,128)(2,1)S(1)}, bf16[4,8,4,1024]{3,2,1,0:T(4,128)(2,1)S(1)}, u32[]{:S(2)}, u32[]{:S(2)}) collective-permute-start(bf16[4,8,4,1024]{3,2,1,0:T(4,128)(2,1)S(1)} %pad_maximum_fusion.2), channel_id=1, source_target_pairs={{0,7},{1,0},{2,1},{3,2},{4,3},{5,4},{6,5},{7,6},{8,15},{9,8},{10,9... | collective-permute-start | bytes 786440 | tf_op jit(solution)/shard_map/ppermute | solution.py:10
  190.4 9.6 %collective-permute-start.2 = (bf16[4,8,4,1024]{3,2,1,0:T(4,128)(2,1)S(1)}, bf16[4,8,4,1024]{3,2,1,0:T(4,128)(2,1)S(1)}, u32[]{:S(2)}, u32[]{:S(2)}) collective-permute-start(bf16[4,8,4,1024]{3,2,1,0:T(4,128)(2,1)S(1)} %slice.46), channel_id=1, source_target_pairs={{0,1},{1,2},{2,3},{3,4},{4,5},{5,6},{6,7},{7,0},{8,9},{9,10},{10,1... | collective-permute-start | bytes 786440 | tf_op jit(solution)/shard_map/ppermute | solution.py:10
  200.0 165.4 %copy-start.3 = (bf16[4,8,32,1024]{3,2,1,0:T(8,128)(2,1)S(1)}, bf16[4,8,32,1024]{3,2,1,0:T(8,128)(2,1)}, u32[]{:S(2)}) copy-start(bf16[4,8,32,1024]{3,2,1,0:T(8,128)(2,1)} %param.9) | copy-start | bytes 6291460
  200.4 13.8 %collective-permute-start.3 = (bf16[4,4,32,1024]{3,2,1,0:T(8,128)(2,1)S(1)}, bf16[4,4,32,1024]{3,2,1,0:T(8,128)(2,1)S(1)}, u32[]{:S(2)}, u32[]{:S(2)}) collective-permute-start(bf16[4,4,32,1024]{3,2,1,0:T(8,128)(2,1)S(1)} %fusion.68), channel_id=1, source_target_pairs={{0,8},{8,16},{16,24},{24,32},{32,40},{40,48},{48,56},{56,64},{64,7... | collective-permute-start | bytes 3145736 | tf_op jit(solution)/shard_map/ppermute | solution.py:10
  370.0 1.4 copy-start.4
  686.5 26.8 %copy-start.1 = (f32[225,16]{0,1:T(8,128)S(1)}, f32[225,16]{0,1:T(8,128)}, u32[]{:S(2)}) copy-start(f32[225,16]{0,1:T(8,128)} %param.14) | copy-start | bytes 43204
Sparse Core Ops, SparseCore 0:
  9.0 356.2 all-gather.2
  367.0 319.4 all-gather.4
